TPU v7x, 1024 devices: a whole 4x8x16 slice. The times are simulated.
1024 devices in a mesh: cuts: 16 (over z_hi, x, core), stem: 64 (over y, z_lo).
Axes of the slice: x: 4, y: 8, z: 16 (z_hi: 2, z_lo: 8; z = z_hi * 8 + z_lo), core: 2. Of those that a mesh axis runs over, the one named last changes fastest.
Arguments:
- stems: bfloat16 [16, 64, 128, 2, 512], P('cuts', 'stem'), may hold values from -6 to 6
- branches: bfloat16 [2, 2, 2, 512, 512], replicated, may hold values from -0.1875 to 0.1875
- closing: bfloat16 [2, 2, 512, 256], replicated, may hold values from -0.046875 to 0.046875
- slice_values: int32 [16, 3], P('cuts'), may hold values from 0 to 1
- mode_perms: int32 [3, 9], replicated, may hold values from 0 to 8, each once within a row
- owner_map: int32 [16], replicated, may hold values from 0 to 15, each once
Outputs:
- open_amplitudes: float32 [64, 16, 2, 16, 128], P('stem', 'cuts')
Inputs may be any that keep to these rules, and one draw needn't show every extreme that they name: `mode_perms`: each row is a permutation of the 9 modes. `owner_map`: a permutation of the owner indices.
All inputs are finite; a program needn't handle non-finite values.
Results may differ from a plain program's by a relative error of at most 0.017.
Values may be sent and summed in bfloat16 or wider, within the bound.
A program may use at most 32 MiB of HBM per device.

v0:
```python
import jax
import jax.numpy as jnp
from jax import lax
from jax.sharding import PartitionSpec as P


def split_up(array, dim, peers):
    lengths = array.shape
    blocks = array.reshape(*lengths[:dim], peers, lengths[dim] // peers, *lengths[dim + 1 :])
    return jnp.moveaxis(blocks, dim, 0)


def sent_and_summed(array, axis, dim):
    peers = lax.axis_size(axis)
    blocks = lax.all_to_all(split_up(array, dim, peers), axis, 0, 0, tiled=True)
    return jnp.sum(blocks.astype(jnp.float32), axis=0)


def inverse_order(perm, width):
    column = jnp.arange(width, dtype=jnp.int32)
    result = jnp.zeros((width,), jnp.int32)
    for bit in range(perm.shape[0]):
        moved = jnp.bitwise_and(jnp.right_shift(column, perm[bit]), 1)
        result = result + jnp.left_shift(moved, bit)
    return result


def complex_block(pair):
    real_part = pair[0]
    imag_part = pair[1]
    top = jnp.concatenate([real_part, imag_part], axis=1)
    bottom = jnp.concatenate([-imag_part, real_part], axis=1)
    return jnp.concatenate([top, bottom], axis=0)


def body(stems, branches, closing, slice_values, mode_perms, owner_map):
    groups = lax.axis_size("stem")
    cuts = lax.axis_size("cuts")
    rows = stems.shape[2]
    width = stems.shape[4]
    half = closing.shape[3]
    high = rows // groups
    narrow = width // groups
    piece_width = half // cuts
    chosen = slice_values[0]
    first_pair = jnp.take(branches[0, chosen[0]], inverse_order(mode_perms[0], width), axis=1)
    second_pair = jnp.take(branches[1, chosen[1]], inverse_order(mode_perms[1], width), axis=1)
    last_pair = jnp.take(closing[chosen[2]], inverse_order(mode_perms[2], width), axis=1)
    last_pair = jnp.take(last_pair.reshape(2, width, cuts, piece_width), owner_map, axis=2)
    first_mat = complex_block(first_pair)
    second_mat = complex_block(second_pair)
    real_last = last_pair[0]
    imag_last = last_pair[1]
    upper = jnp.stack([real_last, imag_last], axis=1)
    lower = jnp.stack([-imag_last, real_last], axis=1)
    last_mat = jnp.stack([upper, lower], axis=0)
    state = stems.reshape(rows, 2 * width)
    begun = jnp.dot(state, first_mat, preferred_element_type=jnp.float32).astype(jnp.bfloat16)
    outgoing = jnp.transpose(begun.reshape(high, groups, 2, groups, narrow), (3, 0, 2, 1, 4))
    piece = lax.all_to_all(outgoing, "stem", split_axis=0, concat_axis=0, tiled=True)
    count = piece.shape[1]
    flat = piece.reshape(groups * count, 2 * width)
    out = jnp.dot(flat, second_mat, preferred_element_type=jnp.float32).astype(jnp.bfloat16)
    mixed = out.reshape(groups, count, 2, width)
    mixed = mixed.reshape(rows, 2, width)
    leaving = jnp.transpose(mixed.reshape(high, groups, 2, groups, narrow), (3, 0, 2, 1, 4))
    arrived = lax.all_to_all(leaving, "stem", split_axis=0, concat_axis=0, tiled=True).reshape(
        rows, 2 * width
    )
    block = last_mat
    block = block.reshape(2 * width, 2, 1 * lax.axis_size("cuts"), piece_width)
    summed = sent_and_summed(
        jnp.einsum("rm,mqbk->bqkr", arrived, block, preferred_element_type=jnp.float32).astype(
            jnp.bfloat16
        ),
        "cuts",
        0,
    )
    return summed.reshape(1, 1, 2, piece_width, rows)


def solution(mesh):
    in_specs = (P("cuts", "stem", None, None, None), P(), P(), P("cuts", None), P(), P())
    out_specs = P("stem", "cuts", None, None, None)
    return jax.shard_map(body, mesh=mesh, in_specs=in_specs, out_specs=out_specs, check_vma=False)
```

profile of v0, /device:TPU:1, one launch (start us, length us, event | category | flops | bytes accessed | tf_op | source)
XLA Modules:
  0.0 179.5 jit_solution(5306188351076668755)
XLA Ops:
  0.0 1.4 fusion.38
  3.8 2.1 %fusion.36 = (s32[1,1]{1,0:T(1,128)}, s32[1,1]{1,0:T(1,128)}, s32[1,1]{1,0:T(1,128)}, s32[1,1]{1,0:T(1,128)}, s32[1,1]{1,0:T(1,128)}, /*index=5*/s32[1,1]{1,0:T(...) fusion(s32[3,9]{1,0:T(4,128)} %param.12), kind=kLoop, calls=%fused_computation.69 | loop fusion | bytes 152 | tf_op jit(solution)/shard_map/slice | solution.py:23
  5.9 5.8 %compare_and_fusion.1 = (pred[512]{0:T(512)(128)(4,1)S(1)}, s32[512]{0:T(512)S(1)}) fusion(s32[]{:T(128)} %bitcast.27, s32[]{:T(128)} %bitcast.26, s32[]{:T(128)} %bitcast.25, s32[]{:T(128)} %bitcast.24, s32[]{:T(128)} %bitcast.23, s32[]{:T(128)} %bitcast.22, s32[]{:T(128)} %bitcast.21, s32[]{:T(128)} %bitcast.20, s32[]{:T(128)} %bitcast.19), kind=kLoop, calls=%fused_computation.56 | loop fusion | flops 20992 | bytes 2596 | tf_op jit(solution)/shard_map/jit(_take)/and | solution.py:46
  12.9 1.7 constant_dynamic-slice_fusion
  14.6 7.5 %copy_bitcast_fusion = (bf16[2,512,512]{2,0,1:T(2,128)(2,1)S(1)}, bf16[2,512,512]{2,0,1:T(2,128)(2,1)}) fusion(bf16[1,1,2,512,512]{4,3,2,1,0:T(8,128)(2,1)S(1)} %get-tuple-element.14, bf16[1,1,2,512,512]{4,3,2,1,0:T(8,128)(2,1)S(1)} %get-tuple-element.15), kind=kLoop, calls=%fused_computation.28 | loop fusion | bytes 4194304 | tf_op jit(solution)/shard_map/squeeze | solution.py:47
  22.1 4.2 %gather_fusion.2 = bf16[512,2,512]{2,1,0:T(2,128)(2,1)S(1)} fusion(bf16[2,512,512]{2,0,1:T(2,128)(2,1)} %get-tuple-element.55, s32[1024]{0:T(1024)S(1)} %pad_clamp_fusion.1), kind=kCustom, calls=%fused_computation.clone | custom fusion | bytes 2099200 | tf_op jit(solution)/shard_map/jit(_take)/gather | solution.py:46
  26.4 2.0 %fusion.26 = bf16[2,512,512]{2,0,1:T(2,128)(2,1)S(1)} fusion(bf16[512,2,512]{2,1,0:T(2,128)(2,1)S(1)} %gather_fusion.2, pred[512]{0:T(512)(128)(4,1)S(1)} %get-tuple-element.12), kind=kLoop, calls=%fused_computation.30 | loop fusion | flops 524288 | bytes 2097664 | tf_op jit(solution)/shard_map/jit(_take)/select_n | solution.py:46
  28.3 1.5 fusion.35
  30.1 0.8 fusion.22
  31.2 1.0 reshape.300
  32.2 22.7 %all-to-all-start = ((bf16[64,2,1024]{2,1,0:T(2,128)(2,1)}), bf16[64,2,1024]{2,1,0:T(2,128)(2,1)S(1)}, u32[]{:S(2)}, u32[]{:S(2)}) async-start(bf16[64,2,1024]{2,1,0:T(2,128)(2,1)} %reshape.300), calls=%async_computation | async-start | bytes 524288 | tf_op jit(solution)/shard_map/all_to_all | solution.py:60
  55.0 0.7 fusion.37
  56.9 5.5 %compare_and_fusion = (pred[512]{0:T(512)(128)(4,1)S(1)}, s32[512]{0:T(512)S(1)}) fusion(s32[]{:T(128)} %bitcast.41, s32[]{:T(128)} %bitcast.40, s32[]{:T(128)} %bitcast.39, s32[]{:T(128)} %bitcast.38, s32[]{:T(128)} %bitcast.37, s32[]{:T(128)} %bitcast.36, s32[]{:T(128)} %bitcast.35, s32[]{:T(128)} %bitcast.34, s32[]{:T(128)} %bitcast.33), kind=kLoop, calls=%fused_computation.55 | loop fusion | flops 20992 | bytes 2596 | tf_op jit(solution)/shard_map/jit(_take)/and | solution.py:47
  62.5 3.6 %gather_fusion.3 = bf16[512,2,512]{2,1,0:T(2,128)(2,1)S(1)} fusion(bf16[2,512,512]{2,0,1:T(2,128)(2,1)S(1)} %get-tuple-element.54, s32[1024]{0:T(1024)S(1)} %pad_clamp_fusion), kind=kCustom, calls=%fused_computation.1.clone | custom fusion | bytes 2099200 | tf_op jit(solution)/shard_map/jit(_take)/gather | solution.py:47
  66.0 2.0 %fusion.27 = bf16[2,512,512]{2,0,1:T(2,128)(2,1)S(1)} fusion(bf16[512,2,512]{2,1,0:T(2,128)(2,1)S(1)} %gather_fusion.3, pred[512]{0:T(512)(128)(4,1)S(1)} %get-tuple-element.8), kind=kLoop, calls=%fused_computation.31 | loop fusion | flops 524288 | bytes 2097664 | tf_op jit(solution)/shard_map/jit(_take)/select_n | solution.py:47
  68.0 1.5 fusion.34
  69.5 0.9 copy.71
  70.4 5.6 %compare_select_fusion = s32[512,1]{0,1:T(1,128)S(1)} fusion(s32[]{:T(128)} %bitcast.8, s32[]{:T(128)} %bitcast.7, s32[]{:T(128)} %bitcast.6, s32[]{:T(128)} %bitcast.5, s32[]{:T(128)} %bitcast.4, s32[]{:T(128)} %bitcast.3, s32[]{:T(128)} %bitcast.2, s32[]{:T(128)} %bitcast.1, s32[]{:T(128)} %bitcast), kind=kLoop, calls=%fused_computation.46 | loop fusion | flops 19456 | bytes 2084 | tf_op jit(solution)/shard_map/jit(_take)/jit(_where)/select_n | solution.py:48
  77.3 3.0 %gather_fusion = bf16[512,2,256]{2,1,0:T(2,128)(2,1)} fusion(bf16[2,512,256]{2,0,1:T(2,128)(2,1)S(1)} %bitcast.116, s32[1024]{0:T(1024)S(1)} %pad_clamp_fusion.3), kind=kCustom, calls=%fused_computation.2 | custom fusion | bytes 1050624 | tf_op jit(solution)/shard_map/jit(_take)/gather | solution.py:48
  80.4 1.3 copy.39
  81.7 5.6 %compare_and_fusion.2 = pred[512]{0:T(512)(128)(4,1)S(1)} fusion(s32[]{:T(128)} %bitcast.8, s32[]{:T(128)} %bitcast.7, s32[]{:T(128)} %bitcast.6, s32[]{:T(128)} %bitcast.5, s32[]{:T(128)} %bitcast.4, s32[]{:T(128)} %bitcast.3, s32[]{:T(128)} %bitcast.2, s32[]{:T(128)} %bitcast.1, s32[]{:T(128)} %bitcast), kind=kLoop, calls=%fused_computation.57 | loop fusion | flops 20992 | bytes 548 | tf_op jit(solution)/shard_map/jit(_take)/and | solution.py:48
  87.4 0.9 fusion.32
  88.7 3.1 %copy.44 = bf16[64,2,2,64,8]{4,3,2,1,0:T(8,128)(2,1)} copy(bf16[64,2,2,64,8]{3,4,2,1,0:T(8,128)(2,1)S(1)} %bitcast.113) | data formatting | bytes 524288 | tf_op jit(solution)/shard_map/all_to_all | solution.py:60
  91.8 7.1 %reshape.255 = bf16[128,1024]{1,0:T(8,128)(2,1)S(1)} reshape(bf16[64,2,2,64,8]{4,3,2,1,0:T(8,128)(2,1)} %copy.44) | data formatting | bytes 524288 | tf_op jit(solution)/shard_map/reshape | solution.py:62
  98.9 1.2 fusion.16
  100.1 1.1 copy.46
  101.8 1.0 reshape.302
  102.8 14.9 %all-to-all-start.1 = ((bf16[64,2,1024]{2,1,0:T(2,128)(2,1)}), bf16[64,2,1024]{2,1,0:T(2,128)(2,1)S(1)}, u32[]{:S(2)}, u32[]{:S(2)}) async-start(bf16[64,2,1024]{2,1,0:T(2,128)(2,1)} %reshape.302), calls=%async_computation.1 | async-start | bytes 524288 | tf_op jit(solution)/shard_map/all_to_all | solution.py:67
  118.9 18.8 %all-to-all-done.1 = bf16[64,2,1024]{2,1,0:T(2,128)(2,1)S(1)} async-done(((bf16[64,2,1024]{2,1,0:T(2,128)(2,1)}), bf16[64,2,1024]{2,1,0:T(2,128)(2,1)S(1)}, u32[]{:S(2)}, u32[]{:S(2)}) %all-to-all-start.1) | async-done | bytes 262176 | tf_op jit(solution)/shard_map/all_to_all | solution.py:67
  138.1 3.2 %copy.48 = bf16[64,2,2,64,8]{4,3,2,1,0:T(8,128)(2,1)} copy(bf16[64,2,2,64,8]{3,1,4,2,0:T(2,128)(2,1)S(1)} %bitcast.114) | data formatting | bytes 524288 | tf_op jit(solution)/shard_map/all_to_all | solution.py:67
  141.2 7.0 %reshape.298 = bf16[128,1024,1,1]{1,0,2,3:T(8,128)(2,1)S(1)} reshape(bf16[64,2,2,64,8]{4,3,2,1,0:T(8,128)(2,1)} %copy.48) | data formatting | bytes 524288 | tf_op jit(solution)/shard_map/reshape | solution.py:67
  148.7 30.2 %all_to_all.15 = bf16[16,1,2,16,128]{4,3,2,1,0:T(8,128)(2,1)S(1)} all-to-all(bf16[16,1,2,16,128]{4,3,2,1,0:T(8,128)(2,1)S(1)} %copy.49), channel_id=1, replica_groups=mesh['cuts'=16,'stem'=64] {'cuts'}, dimensions={0} | all-to-all | bytes 262144 | tf_op jit(solution)/shard_map/all_to_all | solution.py:15
  (41 shorter events, 4.7 us)
Async XLA Ops:
  0.0 76.7 %copy-start = (bf16[2,2,512,256]{3,2,1,0:T(8,128)(2,1)S(1)}, bf16[2,2,512,256]{3,2,1,0:T(8,128)(2,1)}, u32[]{:S(2)}) copy-start(bf16[2,2,512,256]{3,2,1,0:T(8,128)(2,1)} %param.10) | copy-start | bytes 3145732
  28.3 1.7 copy-start.3
  30.1 24.8 %copy-start.4 = (s32[3,9]{1,0:T(4,128)S(1)}, s32[3,9]{1,0:T(4,128)}, u32[]{:S(2)}) copy-start(s32[3,9]{1,0:T(4,128)} %param.12) | copy-start | bytes 328
  32.2 56.1 %all-to-all-start = ((bf16[64,2,1024]{2,1,0:T(2,128)(2,1)}), bf16[64,2,1024]{2,1,0:T(2,128)(2,1)S(1)}, u32[]{:S(2)}, u32[]{:S(2)}) async-start(bf16[64,2,1024]{2,1,0:T(2,128)(2,1)} %reshape.300), calls=%async_computation | async-start | bytes 524288 | tf_op jit(solution)/shard_map/all_to_all | solution.py:60
  68.0 19.3 %copy-start.5 = (s32[16]{0:T(128)S(1)}, s32[16]{0:T(128)}, u32[]{:S(2)}) copy-start(s32[16]{0:T(128)} %param.13) | copy-start | bytes 196
  88.6 10.2 %copy-start.1 = (bf16[1,512,512]{2,1,0:T(8,128)(2,1)S(1)}, bf16[1,512,512]{2,1,0:T(8,128)(2,1)}, u32[]{:S(2)}) copy-start(bf16[1,512,512]{2,1,0:T(8,128)(2,1)} %copy.71) | copy-start | bytes 1572868
  91.8 7.1 %copy-start.2 = (bf16[512,512]{1,0:T(8,128)(2,1)S(1)}, bf16[512,512]{1,0:T(8,128)(2,1)}, u32[]{:S(2)}) copy-start(bf16[512,512]{1,0:T(8,128)(2,1)} %get-tuple-element.7) | copy-start | bytes 1572868
  102.8 34.9 %all-to-all-start.1 = ((bf16[64,2,1024]{2,1,0:T(2,128)(2,1)}), bf16[64,2,1024]{2,1,0:T(2,128)(2,1)S(1)}, u32[]{:S(2)}, u32[]{:S(2)}) async-start(bf16[64,2,1024]{2,1,0:T(2,128)(2,1)} %reshape.302), calls=%async_computation.1 | async-start | bytes 524288 | tf_op jit(solution)/shard_map/all_to_all | solution.py:67
where the time goes:
time: 182 us; the launch traced here: 180 us
  local copies, waits for them, and re-layouts  56.1 us (31%)
  starting transfers between devices  37.6 us (21%)
  blocking collectives  30.2 us (17%)
  other arithmetic  28.5 us (16%)
  waiting for transfers between devices  18.8 us (10%)
  between operations  5.95 us (3%)
  matrix products  2.35 us (1%)
    all_to_all x1, blocking collectives, sent_and_summed(): blocks = lax.all_to_all(split_up(array, dim, peers), axis, 0, 0, tiled=True)  30.2 us
    all_to_all x1, starting transfers between devices, body(): lax.all_to_all(outgoing, 'stem', split_axis=0, concat_axis=0, tiled=True)  22.7 us
    all_to_all x1, waiting for transfers between devices, body(): lax.all_to_all(leaving, 'stem', split_axis=0, concat_axis=0, tiled=True)  18.8 us
    all_to_all x1, starting transfers between devices, body(): lax.all_to_all(leaving, 'stem', split_axis=0, concat_axis=0, tiled=True)  14.9 us
    squeeze x1, local copies, waits for them, and re-layouts, body(): branches[1, chosen[1]]  7.51 us
    reshape x1, local copies, waits for them, and re-layouts, body(): flat = piece.reshape(groups * count, 2 * width)  7.08 us
    reshape x1, local copies, waits for them, and re-layouts, body(): lax.all_to_all(leaving, 'stem', split_axis=0, concat_axis=0, tiled=True)  7.02 us
    and x1, other arithmetic, body(): jnp.take(branches[0, chosen[0]], inverse_order(mode_perms[0], width), axi...  5.76 us
  transfers between devices with their start and end apart: 2, of which 1 were waited for; matrix products, arithmetic and copies ran while one was open for 18% of the time, Pallas kernels for 0%

commit v1 on v0

v1 whole, which is shorter than its diff:
```python
import functools

import jax
import jax.numpy as jnp
from jax import lax
from jax.experimental import pallas as pl
from jax.experimental.pallas import tpu as pltpu
from jax.sharding import PartitionSpec as P


BF = jnp.bfloat16
F32 = jnp.float32
MESH = pl.DeviceIdType.MESH


def group_at(x, co, yy, zz):
    row = (yy + 2 + 4 * (x // 2)) % 8
    col = 2 * (co * 2 + x % 2) + 1 - zz
    return row * 8 + col


def place_of(group):
    row = group // 8
    col = group % 8
    turned = (row + 6) % 8
    zz = 1 - col % 2
    quarter = col // 2
    return (turned // 4) * 2 + quarter % 2, quarter // 2, turned % 4, zz


def spread(index, perms, which):
    total = jnp.zeros_like(index)
    for bit in range(9):
        moved = (index >> bit) & 1
        total = total + moved * (jnp.int32(1) << perms[which, bit])
    return total


def one_hot(rows, cols):
    return jnp.where(rows == cols, 1.0, 0.0).astype(BF)


def iota(shape, dim):
    return lax.broadcasted_iota(jnp.int32, shape, dim)


def mm(a, b):
    return jnp.dot(a, b, preferred_element_type=F32)


def turn(a, shift):
    return pltpu.roll(a, shift % 128, axis=a.ndim - 1)


def fold(direct, crossed, even):
    return direct + jnp.where(even, -turn(crossed, -1), turn(crossed, 1))


def kernel(chosen, perms, owners, x_hbm, br_hbm, cl_hbm, out_ref,
           xv, brv0, brv1, clv, sendbuf, recv1, fbuf, recv2, flag, flags, w3,
           lsem, send1, got1, send2, got2, sendf, gotf):
    cuts = lax.axis_index("cuts")
    stem = lax.axis_index("stem")
    zh, x, co = cuts // 8, (cuts // 2) % 4, cuts % 2
    y, zl = stem // 8, stem % 8
    yh, yy, zp, zz = y // 4, y % 4, zl // 2, zl % 2

    loads = [
        pltpu.make_async_copy(x_hbm, xv, lsem.at[0]),
        pltpu.make_async_copy(br_hbm.at[0], brv0, lsem.at[1]),
        pltpu.make_async_copy(br_hbm.at[1], brv1, lsem.at[2]),
        pltpu.make_async_copy(cl_hbm, clv, lsem.at[3]),
    ]
    for load in loads:
        load.start()

    def mate(step):
        dx, dc, dy, dz = step // 16, (step // 8) % 2, (step // 2) % 4, step % 2
        return (x + dx) % 4, (co + dc) % 2, (yy + dy) % 4, (zz + dz) % 2

    def device(px, pc, py, pz):
        return (zh * 8 + px * 2 + pc, yh * 32 + py * 8 + zp * 2 + pz)

    barrier = pltpu.get_barrier_semaphore()
    qx, qc, qy, qz = place_of(stem)

    def greet_source(pool, carry):
        pzh, pyh, pzp = pool // 8, (pool // 4) % 2, pool % 4
        pl.semaphore_signal(
            barrier, inc=1, device_id=(pzh * 8 + qx * 2 + qc, pyh * 32 + qy * 8 + pzp * 2 + qz), device_id_type=MESH
        )
        return carry

    lax.fori_loop(0, 16, greet_source, 0)

    def greet_mate(step, carry):
        pl.semaphore_signal(barrier, inc=1, device_id=device(*mate(step)), device_id_type=MESH)
        return carry

    lax.fori_loop(1, 64, greet_mate, 0)

    even = iota((1, 128), 1) % 2 == 0
    wide = iota((1, 512), 1)
    tall = iota((512, 512), 0)
    pick0 = one_hot(tall, spread(wide, perms, 0))
    part = iota((256, 256), 0)
    apart = one_hot((part % 128) * 2 + part // 128, iota((256, 256), 1))
    pair = (wide // 128) * 2 + wide % 2
    regroup = one_hot(tall, ((wide % 128) // 2) * 8 + pair)
    pick1 = one_hot((tall % 64) * 8 + tall // 64, spread(wide, perms, 1))

    flag[...] = jnp.full((8, 128), chosen[0, 2], jnp.int32).astype(F32)

    loads[0].wait()
    rows = xv[...].reshape(256, 512)
    rows = mm(apart, rows).astype(BF)
    rows = mm(rows, pick0).astype(BF)
    loads[1].wait()
    v0 = chosen[0, 0]
    y0 = mm(rows, brv0[v0, 0])
    y1 = mm(rows, brv0[v0, 1])
    a1 = jnp.concatenate([y0[:128] - y1[128:], y1[:128] + y0[128:]], axis=0).astype(BF)
    t = mm(a1, regroup)

    blocks = []
    for e2 in range(4):
        lanes = slice(e2 * 128, e2 * 128 + 128)
        low, high = [], []
        for h in range(2):
            re = t[h * 64:h * 64 + 64, lanes]
            im = t[128 + h * 64:192 + h * 64, lanes]
            low.append(jnp.where(even, re, turn(im, 1)))
            high.append(jnp.where(even, turn(re, -1), im))
        blocks.append(jnp.concatenate(low, axis=1))
        blocks.append(jnp.concatenate(high, axis=1))
    z = jnp.concatenate(blocks, axis=0).astype(BF)
    zq = lax.dot_general(pick1, z, (((0,), (0,)), ((), ())), preferred_element_type=F32).astype(BF)

    loads[2].wait()
    v1 = chosen[0, 1]
    t0 = lax.dot_general(brv1[v1, 0], zq, (((0,), (0,)), ((), ())), preferred_element_type=F32)
    t1 = lax.dot_general(brv1[v1, 1], zq, (((0,), (0,)), ((), ())), preferred_element_type=F32)
    halves = [
        fold(t0[:, h * 128:h * 128 + 128], t1[:, h * 128:h * 128 + 128], even).reshape(64, 8, 128) for h in range(2)
    ]
    sendbuf[...] = jnp.concatenate(halves, axis=1).astype(BF)

    pl.semaphore_wait(barrier, 79)

    mine = x * 2 + co

    def send_flag(step, carry):
        px, pc = (x + step // 2) % 4, (co + step % 2) % 2
        pltpu.make_async_remote_copy(
            src_ref=flag, dst_ref=flags.at[mine], send_sem=sendf, recv_sem=gotf,
            device_id=device(px, pc, yy, zz), device_id_type=MESH,
        ).start()
        return carry

    lax.fori_loop(1, 8, send_flag, 0)

    slot = mine * 8 + yy * 2 + zz

    def send_block(step, carry):
        px, pc, py, pz = mate(step)
        pltpu.make_async_remote_copy(
            src_ref=sendbuf.at[group_at(px, pc, py, pz)], dst_ref=recv1.at[slot], send_sem=send1, recv_sem=got1,
            device_id=device(px, pc, py, pz), device_id_type=MESH,
        ).start()
        return carry

    lax.fori_loop(1, 64, send_block, 0)
    recv1[slot] = sendbuf[group_at(x, co, yy, zz)]
    flags[mine] = flag[...]

    loads[3].wait()
    sub = iota((128, 512), 0)
    source = (((sub // 32) * 8 + zp * 2 + (sub // 16) % 2) * 2 + (sub // 8) % 2) * 8 + sub % 8
    pick2 = one_hot(source, spread(wide, perms, 2))
    column = iota((256, 256), 1)
    owner = jnp.zeros((1, 256), jnp.int32)
    block_of = iota((1, 256), 1) // 16
    for b in range(16):
        owner = jnp.where(block_of == b, owners[b], owner)
    deal = one_hot(iota((256, 256), 0), owner * 16 + iota((1, 256), 1) % 16)
    both = []
    for v in range(2):
        parts = [mm(mm(pick2, clv[v, q]).astype(BF), deal) for q in range(2)]
        both.append(jnp.concatenate(parts, axis=1).T)
    pltpu.make_async_copy(flags.at[pl.ds(0, 7)], flags.at[pl.ds(0, 7)], gotf).wait()
    for c in range(8):
        on = jnp.broadcast_to(flags[c][:1], (512, 128)) > 0.5
        w3[:, c * 128:c * 128 + 128] = jnp.where(on, both[1], both[0]).astype(BF)

    pltpu.make_async_copy(recv1.at[pl.ds(0, 63)], recv1.at[pl.ds(0, 63)], got1).wait()
    f = mm(w3[...], recv1[...].reshape(1024, 128))
    fbuf[...] = fold(f[:256], f[256:], even).reshape(16, 16, 128).astype(BF)

    group = group_at(x, co, yy, zz)
    pool = zh * 8 + yh * 4 + zp

    def send_part(step, carry):
        b = (cuts + 15 - step) % 16
        pltpu.make_async_remote_copy(
            src_ref=fbuf.at[b], dst_ref=recv2.at[pool], send_sem=send2, recv_sem=got2,
            device_id=(b, group), device_id_type=MESH,
        ).start()
        return carry

    lax.fori_loop(0, 16, send_part, 0)
    pltpu.make_async_copy(recv2, recv2, got2).wait()
    sums = []
    for h in range(2):
        total = jnp.zeros((16, 128), F32)
        for z2 in range(2):
            for k in range(4):
                total = total + recv2[z2 * 8 + h * 4 + k].astype(F32)
        sums.append(total)
    out_ref[0] = jnp.where(even, sums[0], turn(sums[1], 1))
    out_ref[1] = jnp.where(even, turn(sums[0], -1), sums[1])

    pltpu.make_async_copy(flags.at[pl.ds(0, 7)], flags.at[pl.ds(0, 7)], sendf).wait()
    pltpu.make_async_copy(sendbuf.at[pl.ds(0, 63)], sendbuf.at[pl.ds(0, 63)], send1).wait()
    pltpu.make_async_copy(fbuf, fbuf, send2).wait()


def body(stems, branches, closing, slice_values, mode_perms, owner_map):
    smem = pl.BlockSpec(memory_space=pltpu.SMEM)
    hbm = pl.BlockSpec(memory_space=pl.ANY)
    out = pl.pallas_call(
        kernel,
        out_shape=jax.ShapeDtypeStruct((2, 16, 128), F32),
        in_specs=[smem, smem, smem, hbm, hbm, hbm],
        out_specs=pl.BlockSpec(memory_space=pltpu.VMEM),
        scratch_shapes=[
            pltpu.VMEM((128, 2, 512), BF),
            pltpu.VMEM((2, 2, 512, 512), BF),
            pltpu.VMEM((2, 2, 512, 512), BF),
            pltpu.VMEM((2, 2, 512, 256), BF),
            pltpu.VMEM((64, 16, 128), BF),
            pltpu.VMEM((64, 16, 128), BF),
            pltpu.VMEM((16, 16, 128), BF),
            pltpu.VMEM((16, 16, 128), BF),
            pltpu.VMEM((8, 128), F32),
            pltpu.VMEM((8, 8, 128), F32),
            pltpu.VMEM((512, 1024), BF),
            pltpu.SemaphoreType.DMA((4,)),
            pltpu.SemaphoreType.DMA,
            pltpu.SemaphoreType.DMA,
            pltpu.SemaphoreType.DMA,
            pltpu.SemaphoreType.DMA,
            pltpu.SemaphoreType.DMA,
            pltpu.SemaphoreType.DMA,
        ],
        compiler_params=pltpu.CompilerParams(collective_id=0, has_side_effects=True),
    )(slice_values, mode_perms, owner_map, stems.reshape(128, 2, 512), branches, closing)
    return out.reshape(1, 1, 2, 16, 128)


def solution(mesh):
    in_specs = (P("cuts", "stem", None, None, None), P(), P(), P("cuts", None), P(), P())
    out_specs = P("stem", "cuts", None, None, None)
    return jax.shard_map(body, mesh=mesh, in_specs=in_specs, out_specs=out_specs, check_vma=False)
```

time: 182 us -> 48.6 us (0.27); the launches traced: 180 us -> 48.3 us
  local copies, waits for them, and re-layouts: 56.1 us -> 1.32 us
  Pallas kernels: 0 us -> 47 us
  starting transfers between devices: 37.6 us -> 0 us
  blocking collectives: 30.2 us -> 0 us
  other arithmetic: 28.5 us -> 0 us
  waiting for transfers between devices: 18.8 us -> 0 us
  between operations: 5.95 us -> 0.01 us
  matrix products: 2.35 us -> 0 us
    pallas_call x0 -> x1, Pallas kernels: none -> 47 us  [body(): pl.pallas_call(kernel, out_shape=jax.ShapeDtypeStruct((2, 16, 128), F32),...]
    all_to_all x2 -> x0, starting transfers between devices: 37.6 us -> none  [the longest x1 22.7 us: body(): lax.all_to_all(outgoing, 'stem', split_axis=0, concat_axis=0, tiled=True)]
    all_to_all x1 -> x0, blocking collectives: 30.2 us -> none  [sent_and_summed(): blocks = lax.all_to_all(split_up(array, dim, peers), axis, 0, 0, tiled=True)]
    all_to_all x2 -> x0, waiting for transfers between devices: 18.8 us -> none  [the longest x1 18.8 us: body(): lax.all_to_all(leaving, 'stem', split_axis=0, concat_axis=0, tiled=True)]
    and x4 -> x0, other arithmetic: 16.9 us -> none  [the longest x1 5.76 us: body(): jnp.take(branches[0, chosen[0]], inverse_order(mode_perms[0], width), axi...]
    reshape x6 -> x0, local copies, waits for them, and re-layouts: 14.6 us -> none  [the longest x1 7.08 us: body(): flat = piece.reshape(groups * count, 2 * width)]
    gather x5 -> x0, local copies, waits for them, and re-layouts: 12.7 us -> none  [the longest x2 4.32 us: body(): jnp.take(closing[chosen[2]], inverse_order(mode_perms[2], width), axis=1)]
    select_n x6 -> x0, other arithmetic: 9.75 us -> none  [the longest x2 5.7 us: body(): jnp.take(closing[chosen[2]], inverse_order(mode_perms[2], width), axis=1)]
  transfers between devices with their start and end apart: 2 -> 0, of which waited for: 1 -> 0; matrix products, arithmetic and copies ran while one was open for 18% -> 0% of each run, Pallas kernels for 0% -> 0%
where the time goes in v1:
time: 48.6 us; the launch traced here: 48.3 us
  Pallas kernels  47 us (97%)
  local copies, waits for them, and re-layouts  1.32 us (3%)
    pallas_call x1, Pallas kernels, body(): pl.pallas_call(kernel, out_shape=jax.ShapeDtypeStruct((2, 16, 128), F32),...  47 us
    unnamed x1, local copies, waits for them, and re-layouts  1.32 us

profile of v1, /device:TPU:1, one launch (start us, length us, event | category | flops | bytes accessed | tf_op | source)
XLA Modules:
  0.0 48.3 jit_solution(8764848707849188799)
XLA Ops:
  0.0 47.0 %shard_map.64 = f32[2,16,128]{2,1,0:T(8,128)} custom-call(s32[1,3]{1,0:T(1,128)} %chosen.1, s32[3,9]{1,0:T(4,128)} %perms.1, s32[16]{0:T(128)} %owners.1, bf16[128,2,512]{2,1,0:T(2,128)(2,1)} %bitcast.2, bf16[2,2,2,512,512]{4,3,2,1,0:T(8,128)(2,1)} %br_hbm.1, bf16[2,2,512,256]{3,2,1,0:T(8,128)(2,1)} %cl_hbm.1), custom_call_target="tpu_custom_call" | custom-call | tf_op jit(solution)/shard_map/pallas_call | solution.py:230
  47.0 1.3 %copy.8 = f32[1,1,2,16,128]{4,3,2,1,0:T(8,128)} copy(f32[1,1,2,16,128]{4,3,2,1,0:T(8,128)} %bitcast.3) | data formatting | bytes 32768

commit v2 on v1

--- a/solution.py
+++ b/solution.py
@@ -11,6 +11,9 @@
 BF = jnp.bfloat16
 F32 = jnp.float32
 MESH = pl.DeviceIdType.MESH
+
+FAR_FIRST = [(2, 2), (2, 1), (2, 3), (1, 2), (3, 2), (1, 1), (1, 3), (3, 1), (3, 3),
+             (2, 0), (1, 0), (3, 0), (0, 2), (0, 1), (0, 3), (0, 0)]
 
 
 def group_at(x, co, yy, zz):
@@ -74,30 +77,24 @@
     for load in loads:
         load.start()
 
-    def mate(step):
-        dx, dc, dy, dz = step // 16, (step // 8) % 2, (step // 2) % 4, step % 2
-        return (x + dx) % 4, (co + dc) % 2, (yy + dy) % 4, (zz + dz) % 2
-
-    def device(px, pc, py, pz):
-        return (zh * 8 + px * 2 + pc, yh * 32 + py * 8 + zp * 2 + pz)
+    xs = [lax.rem(x + d, 4) for d in range(4)]
+    cs = [co, 1 - co]
+    ys = [lax.rem(yy + d, 4) for d in range(4)]
+    zs = [zz, 1 - zz]
+    cut_of = [[zh * 8 + px * 2 + pc for pc in cs] for px in xs]
+    stem_of = [[yh * 32 + py * 8 + zp * 2 + pz for pz in zs] for py in ys]
+    mates = [(dx, dy, dc, dz) for dx, dy in FAR_FIRST for dc in (1, 0) for dz in (1, 0)][:-1]
 
     barrier = pltpu.get_barrier_semaphore()
     qx, qc, qy, qz = place_of(stem)
-
-    def greet_source(pool, carry):
-        pzh, pyh, pzp = pool // 8, (pool // 4) % 2, pool % 4
-        pl.semaphore_signal(
-            barrier, inc=1, device_id=(pzh * 8 + qx * 2 + qc, pyh * 32 + qy * 8 + pzp * 2 + qz), device_id_type=MESH
-        )
-        return carry
-
-    lax.fori_loop(0, 16, greet_source, 0)
-
-    def greet_mate(step, carry):
-        pl.semaphore_signal(barrier, inc=1, device_id=device(*mate(step)), device_id_type=MESH)
-        return carry
-
-    lax.fori_loop(1, 64, greet_mate, 0)
+    for pzh in range(2):
+        for pyh in range(2):
+            for pzp in range(4):
+                there = (pzh * 8 + qx * 2 + qc, pyh * 32 + qy * 8 + pzp * 2 + qz)
+                pl.semaphore_signal(barrier, inc=1, device_id=there, device_id_type=MESH)
+    for dx, dy, dc, dz in mates:
+        there = (cut_of[dx][dc], stem_of[dy][dz])
+        pl.semaphore_signal(barrier, inc=1, device_id=there, device_id_type=MESH)
 
     even = iota((1, 128), 1) % 2 == 0
     wide = iota((1, 512), 1)
@@ -149,27 +146,22 @@
 
     mine = x * 2 + co
 
-    def send_flag(step, carry):
-        px, pc = (x + step // 2) % 4, (co + step % 2) % 2
+    slot = mine * 8 + yy * 2 + zz
+    for dx, dc in ((2, 1), (2, 0), (1, 1), (1, 0), (3, 1), (3, 0), (0, 1)):
         pltpu.make_async_remote_copy(
             src_ref=flag, dst_ref=flags.at[mine], send_sem=sendf, recv_sem=gotf,
-            device_id=device(px, pc, yy, zz), device_id_type=MESH,
+            device_id=(cut_of[dx][dc], stem_of[0][0]), device_id_type=MESH,
         ).start()
-        return carry
-
-    lax.fori_loop(1, 8, send_flag, 0)
-
-    slot = mine * 8 + yy * 2 + zz
-
-    def send_block(step, carry):
-        px, pc, py, pz = mate(step)
+    halves_of = [px // 2 for px in xs]
+    cols = [[4 * pc + 2 * (px - 2 * half) + 1 for pc in cs] for px, half in zip(xs, halves_of)]
+    rows_of = [lax.rem(py + 2, 8) * 8 for py in ys]
+    flips = [lax.rem(py + 6, 8) * 8 - row for py, row in zip(ys, rows_of)]
+    for dx, dy, dc, dz in mates:
+        theirs = rows_of[dy] + halves_of[dx] * flips[dy] + cols[dx][dc] - zs[dz]
         pltpu.make_async_remote_copy(
-            src_ref=sendbuf.at[group_at(px, pc, py, pz)], dst_ref=recv1.at[slot], send_sem=send1, recv_sem=got1,
-            device_id=device(px, pc, py, pz), device_id_type=MESH,
+            src_ref=sendbuf.at[theirs], dst_ref=recv1.at[slot], send_sem=send1, recv_sem=got1.at[dx],
+            device_id=(cut_of[dx][dc], stem_of[dy][dz]), device_id_type=MESH,
         ).start()
-        return carry
-
-    lax.fori_loop(1, 64, send_block, 0)
     recv1[slot] = sendbuf[group_at(x, co, yy, zz)]
     flags[mine] = flag[...]
 
@@ -190,24 +182,28 @@
     pltpu.make_async_copy(flags.at[pl.ds(0, 7)], flags.at[pl.ds(0, 7)], gotf).wait()
     for c in range(8):
         on = jnp.broadcast_to(flags[c][:1], (512, 128)) > 0.5
-        w3[:, c * 128:c * 128 + 128] = jnp.where(on, both[1], both[0]).astype(BF)
-
-    pltpu.make_async_copy(recv1.at[pl.ds(0, 63)], recv1.at[pl.ds(0, 63)], got1).wait()
-    f = mm(w3[...], recv1[...].reshape(1024, 128))
+        w3[c // 2, :, (c % 2) * 128:(c % 2) * 128 + 128] = jnp.where(on, both[1], both[0]).astype(BF)
+
+    f = None
+    for dx in (2, 1, 3, 0):
+        px = xs[(4 - dx) % 4]
+        came = recv1.at[pl.ds(px * 16, 16 if dx else 15)]
+        pltpu.make_async_copy(came, came, got1.at[dx]).wait()
+        term = mm(w3[px], recv1[pl.ds(px * 16, 16)].reshape(256, 128))
+        f = term if f is None else f + term
     fbuf[...] = fold(f[:256], f[256:], even).reshape(16, 16, 128).astype(BF)
 
     group = group_at(x, co, yy, zz)
     pool = zh * 8 + yh * 4 + zp
 
-    def send_part(step, carry):
-        b = (cuts + 15 - step) % 16
-        pltpu.make_async_remote_copy(
-            src_ref=fbuf.at[b], dst_ref=recv2.at[pool], send_sem=send2, recv_sem=got2,
-            device_id=(b, group), device_id_type=MESH,
-        ).start()
-        return carry
-
-    lax.fori_loop(0, 16, send_part, 0)
+    for pzh in range(2):
+        for dx in (2, 1, 3, 0):
+            for dc in (1, 0):
+                b = pzh * 8 + xs[dx] * 2 + cs[dc]
+                pltpu.make_async_remote_copy(
+                    src_ref=fbuf.at[b], dst_ref=recv2.at[pool], send_sem=send2, recv_sem=got2,
+                    device_id=(b, group), device_id_type=MESH,
+                ).start()
     pltpu.make_async_copy(recv2, recv2, got2).wait()
     sums = []
     for h in range(2):
@@ -243,10 +239,10 @@
             pltpu.VMEM((16, 16, 128), BF),
             pltpu.VMEM((8, 128), F32),
             pltpu.VMEM((8, 8, 128), F32),
-            pltpu.VMEM((512, 1024), BF),
+            pltpu.VMEM((4, 512, 256), BF),
             pltpu.SemaphoreType.DMA((4,)),
             pltpu.SemaphoreType.DMA,
-            pltpu.SemaphoreType.DMA,
+            pltpu.SemaphoreType.DMA((4,)),
             pltpu.SemaphoreType.DMA,
             pltpu.SemaphoreType.DMA,
             pltpu.SemaphoreType.DMA,

time: 48.6 us -> 46 us (0.947)
  Pallas kernels: 47 us -> 44.5 us
    pallas_call x1, Pallas kernels: 47 us -> 44.5 us  [body(): pl.pallas_call(kernel, out_shape=jax.ShapeDtypeStruct((2, 16, 128), F32),...]
where the time goes in v2:
time: 46 us; the launch traced here: 45.8 us
  Pallas kernels  44.5 us (97%)
  local copies, waits for them, and re-layouts  1.32 us (3%)
    pallas_call x1, Pallas kernels, body(): pl.pallas_call(kernel, out_shape=jax.ShapeDtypeStruct((2, 16, 128), F32),...  44.5 us
    unnamed x1, local copies, waits for them, and re-layouts  1.32 us

profile of v2, /device:TPU:1, one launch (start us, length us, event | category | flops | bytes accessed | tf_op | source)
XLA Modules:
  0.0 45.8 jit_solution(15749242473921267436)
XLA Ops:
  0.0 44.5 %shard_map.64 = f32[2,16,128]{2,1,0:T(8,128)} custom-call(s32[1,3]{1,0:T(1,128)} %chosen.1, s32[3,9]{1,0:T(4,128)} %perms.1, s32[16]{0:T(128)} %owners.1, bf16[128,2,512]{2,1,0:T(2,128)(2,1)} %bitcast.2, bf16[2,2,2,512,512]{4,3,2,1,0:T(8,128)(2,1)} %br_hbm.1, bf16[2,2,512,256]{3,2,1,0:T(8,128)(2,1)} %cl_hbm.1), custom_call_target="tpu_custom_call" | custom-call | tf_op jit(solution)/shard_map/pallas_call | solution.py:226
  44.5 1.3 %copy.8 = f32[1,1,2,16,128]{4,3,2,1,0:T(8,128)} copy(f32[1,1,2,16,128]{4,3,2,1,0:T(8,128)} %bitcast.3) | data formatting | bytes 32768

commit v3 on v2

--- a/solution.py
+++ b/solution.py
@@ -59,9 +59,9 @@
     return direct + jnp.where(even, -turn(crossed, -1), turn(crossed, 1))
 
 
-def kernel(chosen, perms, owners, x_hbm, br_hbm, cl_hbm, out_ref,
-           xv, brv0, brv1, clv, sendbuf, recv1, fbuf, recv2, flag, flags, w3,
-           lsem, send1, got1, send2, got2, sendf, gotf):
+def kernel(chosen_hbm, perms_hbm, owners_hbm, x_hbm, br_hbm, cl_hbm, out_ref,
+           xv, brv0, brv1, clv, sendbuf, recv1, fbuf, recv2, flag, flags, w3, chosen, perms, owners,
+           lsem, send1, got1, send2, got2, sendf, gotf, ready):
     cuts = lax.axis_index("cuts")
     stem = lax.axis_index("stem")
     zh, x, co = cuts // 8, (cuts // 2) % 4, cuts % 2
@@ -74,7 +74,12 @@
         pltpu.make_async_copy(br_hbm.at[1], brv1, lsem.at[2]),
         pltpu.make_async_copy(cl_hbm, clv, lsem.at[3]),
     ]
-    for load in loads:
+    tables = [
+        pltpu.make_async_copy(chosen_hbm, chosen, lsem.at[4]),
+        pltpu.make_async_copy(perms_hbm, perms, lsem.at[5]),
+        pltpu.make_async_copy(owners_hbm, owners, lsem.at[6]),
+    ]
+    for load in tables + loads:
         load.start()
 
     xs = [lax.rem(x + d, 4) for d in range(4)]
@@ -87,15 +92,36 @@
 
     barrier = pltpu.get_barrier_semaphore()
     qx, qc, qy, qz = place_of(stem)
-    for pzh in range(2):
-        for pyh in range(2):
-            for pzp in range(4):
+    height = zh * 8 + zl
+    group = group_at(x, co, yy, zz)
+    owner_z = [lax.rem(group, 8), lax.rem(group, 8) + 8]
+    source_z = [(pzh, pzp, pzh * 8 + pzp * 2 + qz) for pzh in range(2) for pzp in range(4)]
+    due = jnp.int32(63)
+    for pzh, pzp, there_z in source_z:
+        due = due + jnp.where(there_z < height, 2, 0)
+
+        @pl.when(there_z > height)
+        def _(pzh=pzh, pzp=pzp):
+            for pyh in range(2):
                 there = (pzh * 8 + qx * 2 + qc, pyh * 32 + qy * 8 + pzp * 2 + qz)
                 pl.semaphore_signal(barrier, inc=1, device_id=there, device_id_type=MESH)
+
+    for pzh in range(2):
+        due = due + jnp.where(owner_z[pzh] < height, 8, 0)
+
+        @pl.when(owner_z[pzh] > height)
+        def _(pzh=pzh):
+            for px in xs:
+                for pc in cs:
+                    there = (pzh * 8 + px * 2 + pc, group)
+                    pl.semaphore_signal(barrier, inc=1, device_id=there, device_id_type=MESH)
+
     for dx, dy, dc, dz in mates:
         there = (cut_of[dx][dc], stem_of[dy][dz])
         pl.semaphore_signal(barrier, inc=1, device_id=there, device_id_type=MESH)
 
+    for table in tables:
+        table.wait()
     even = iota((1, 128), 1) % 2 == 0
     wide = iota((1, 512), 1)
     tall = iota((512, 512), 0)
@@ -142,7 +168,7 @@
     ]
     sendbuf[...] = jnp.concatenate(halves, axis=1).astype(BF)
 
-    pl.semaphore_wait(barrier, 79)
+    pl.semaphore_wait(barrier, due)
 
     mine = x * 2 + co
 
@@ -162,7 +188,15 @@
             src_ref=sendbuf.at[theirs], dst_ref=recv1.at[slot], send_sem=send1, recv_sem=got1.at[dx],
             device_id=(cut_of[dx][dc], stem_of[dy][dz]), device_id_type=MESH,
         ).start()
-    recv1[slot] = sendbuf[group_at(x, co, yy, zz)]
+    for pzh, pzp, there_z in source_z:
+
+        @pl.when(there_z < height)
+        def _(pzh=pzh, pzp=pzp):
+            for pyh in range(2):
+                there = (pzh * 8 + qx * 2 + qc, pyh * 32 + qy * 8 + pzp * 2 + qz)
+                pl.semaphore_signal(ready.at[zh], inc=1, device_id=there, device_id_type=MESH)
+
+    recv1[slot] = sendbuf[group]
     flags[mine] = flag[...]
 
     loads[3].wait()
@@ -193,10 +227,14 @@
         f = term if f is None else f + term
     fbuf[...] = fold(f[:256], f[256:], even).reshape(16, 16, 128).astype(BF)
 
-    group = group_at(x, co, yy, zz)
     pool = zh * 8 + yh * 4 + zp
 
     for pzh in range(2):
+
+        @pl.when(owner_z[pzh] > height)
+        def _(pzh=pzh):
+            pl.semaphore_wait(ready.at[pzh], 8)
+
         for dx in (2, 1, 3, 0):
             for dc in (1, 0):
                 b = pzh * 8 + xs[dx] * 2 + cs[dc]
@@ -221,12 +259,11 @@
 
 
 def body(stems, branches, closing, slice_values, mode_perms, owner_map):
-    smem = pl.BlockSpec(memory_space=pltpu.SMEM)
     hbm = pl.BlockSpec(memory_space=pl.ANY)
     out = pl.pallas_call(
         kernel,
         out_shape=jax.ShapeDtypeStruct((2, 16, 128), F32),
-        in_specs=[smem, smem, smem, hbm, hbm, hbm],
+        in_specs=[hbm] * 6,
         out_specs=pl.BlockSpec(memory_space=pltpu.VMEM),
         scratch_shapes=[
             pltpu.VMEM((128, 2, 512), BF),
@@ -240,13 +277,17 @@
             pltpu.VMEM((8, 128), F32),
             pltpu.VMEM((8, 8, 128), F32),
             pltpu.VMEM((4, 512, 256), BF),
+            pltpu.SMEM((1, 3), jnp.int32),
+            pltpu.SMEM((3, 9), jnp.int32),
+            pltpu.SMEM((16,), jnp.int32),
+            pltpu.SemaphoreType.DMA((7,)),
+            pltpu.SemaphoreType.DMA,
             pltpu.SemaphoreType.DMA((4,)),
             pltpu.SemaphoreType.DMA,
-            pltpu.SemaphoreType.DMA((4,)),
-            pltpu.SemaphoreType.DMA,
-            pltpu.SemaphoreType.DMA,
-            pltpu.SemaphoreType.DMA,
-            pltpu.SemaphoreType.DMA,
+            pltpu.SemaphoreType.DMA,
+            pltpu.SemaphoreType.DMA,
+            pltpu.SemaphoreType.DMA,
+            pltpu.SemaphoreType.REGULAR((2,)),
         ],
         compiler_params=pltpu.CompilerParams(collective_id=0, has_side_effects=True),
     )(slice_values, mode_perms, owner_map, stems.reshape(128, 2, 512), branches, closing)

time: 46 us -> 43 us (0.935)
  Pallas kernels: 44.5 us -> 41.4 us
    pallas_call x1, Pallas kernels: 44.5 us -> 41.4 us  [body(): pl.pallas_call(kernel, out_shape=jax.ShapeDtypeStruct((2, 16, 128), F32),...]
where the time goes in v3:
time: 43 us; the launch traced here: 42.8 us
  Pallas kernels  41.4 us (96%)
  local copies, waits for them, and re-layouts  1.32 us (3%)
    pallas_call x1, Pallas kernels, body(): pl.pallas_call(kernel, out_shape=jax.ShapeDtypeStruct((2, 16, 128), F32),...  41.4 us
    unnamed x1, local copies, waits for them, and re-layouts  1.32 us

profile of v3, /device:TPU:1, one launch (start us, length us, event | category | flops | bytes accessed | tf_op | source)
XLA Modules:
  0.0 42.8 jit_solution(4477414753901998422)
XLA Ops:
  0.0 41.4 %shard_map.64 = f32[2,16,128]{2,1,0:T(8,128)} custom-call(s32[1,3]{1,0:T(1,128)} %chosen_hbm.1, s32[3,9]{1,0:T(4,128)} %perms_hbm.1, s32[16]{0:T(128)} %owners_hbm.1, bf16[128,2,512]{2,1,0:T(2,128)(2,1)} %bitcast.2, bf16[2,2,2,512,512]{4,3,2,1,0:T(8,128)(2,1)} %br_hbm.1, bf16[2,2,512,256]{3,2,1,0:T(8,128)(2,1)} %cl_hbm.1), custom_call_target="tpu_custom_call" | custom-call | tf_op jit(solution)/shard_map/pallas_call | solution.py:263
  41.5 1.3 %copy.8 = f32[1,1,2,16,128]{4,3,2,1,0:T(8,128)} copy(f32[1,1,2,16,128]{4,3,2,1,0:T(8,128)} %bitcast.3) | data formatting | bytes 32768

commit v4 on v3

--- a/solution.py
+++ b/solution.py
@@ -11,9 +11,6 @@
 BF = jnp.bfloat16
 F32 = jnp.float32
 MESH = pl.DeviceIdType.MESH
-
-FAR_FIRST = [(2, 2), (2, 1), (2, 3), (1, 2), (3, 2), (1, 1), (1, 3), (3, 1), (3, 3),
-             (2, 0), (1, 0), (3, 0), (0, 2), (0, 1), (0, 3), (0, 0)]
 
 
 def group_at(x, co, yy, zz):
@@ -61,7 +58,7 @@
 
 def kernel(chosen_hbm, perms_hbm, owners_hbm, x_hbm, br_hbm, cl_hbm, out_ref,
            xv, brv0, brv1, clv, sendbuf, recv1, fbuf, recv2, flag, flags, w3, chosen, perms, owners,
-           lsem, send1, got1, send2, got2, sendf, gotf, ready):
+           lsem, send1, got1, send2, got2, sendf, gotf, ready, open1):
     cuts = lax.axis_index("cuts")
     stem = lax.axis_index("stem")
     zh, x, co = cuts // 8, (cuts // 2) % 4, cuts % 2
@@ -88,7 +85,8 @@
     zs = [zz, 1 - zz]
     cut_of = [[zh * 8 + px * 2 + pc for pc in cs] for px in xs]
     stem_of = [[yh * 32 + py * 8 + zp * 2 + pz for pz in zs] for py in ys]
-    mates = [(dx, dy, dc, dz) for dx, dy in FAR_FIRST for dc in (1, 0) for dz in (1, 0)][:-1]
+    crowd = [(dx, dc, dz) for dx in (2, 1, 3, 0) for dc in (1, 0) for dz in (1, 0)]
+    rank_of = [jnp.where(yh == 0, py, 3 - py) for py in ys]
 
     barrier = pltpu.get_barrier_semaphore()
     qx, qc, qy, qz = place_of(stem)
@@ -96,7 +94,7 @@
     group = group_at(x, co, yy, zz)
     owner_z = [lax.rem(group, 8), lax.rem(group, 8) + 8]
     source_z = [(pzh, pzp, pzh * 8 + pzp * 2 + qz) for pzh in range(2) for pzp in range(4)]
-    due = jnp.int32(63)
+    due = jnp.int32(15)
     for pzh, pzp, there_z in source_z:
         due = due + jnp.where(there_z < height, 2, 0)
 
@@ -116,9 +114,15 @@
                     there = (pzh * 8 + px * 2 + pc, group)
                     pl.semaphore_signal(barrier, inc=1, device_id=there, device_id_type=MESH)
 
-    for dx, dy, dc, dz in mates:
-        there = (cut_of[dx][dc], stem_of[dy][dz])
-        pl.semaphore_signal(barrier, inc=1, device_id=there, device_id_type=MESH)
+    for dx, dc, dz in crowd[:-1]:
+        pl.semaphore_signal(barrier, inc=1, device_id=(cut_of[dx][dc], stem_of[0][dz]), device_id_type=MESH)
+    for dy in (1, 2, 3):
+        due = due + jnp.where(rank_of[dy] < rank_of[0], 16, 0)
+
+        @pl.when(rank_of[dy] > rank_of[0])
+        def _(dy=dy):
+            for dx, dc, dz in crowd:
+                pl.semaphore_signal(barrier, inc=1, device_id=(cut_of[dx][dc], stem_of[dy][dz]), device_id_type=MESH)
 
     for table in tables:
         table.wait()
@@ -159,6 +163,31 @@
     z = jnp.concatenate(blocks, axis=0).astype(BF)
     zq = lax.dot_general(pick1, z, (((0,), (0,)), ((), ())), preferred_element_type=F32).astype(BF)
 
+    pl.semaphore_wait(barrier, due)
+    for dy in (1, 2, 3):
+
+        @pl.when(rank_of[dy] < rank_of[0])
+        def _(dy=dy):
+            for dx, dc, dz in crowd:
+                there = (cut_of[dx][dc], stem_of[dy][dz])
+                pl.semaphore_signal(open1.at[4 - dy], inc=1, device_id=there, device_id_type=MESH)
+
+    mine = x * 2 + co
+
+    for dx, dc in ((2, 1), (2, 0), (1, 1), (1, 0), (3, 1), (3, 0), (0, 1)):
+        pltpu.make_async_remote_copy(
+            src_ref=flag, dst_ref=flags.at[mine], send_sem=sendf, recv_sem=gotf,
+            device_id=(cut_of[dx][dc], stem_of[0][0]), device_id_type=MESH,
+        ).start()
+
+    for pzh, pzp, there_z in source_z:
+
+        @pl.when(there_z < height)
+        def _(pzh=pzh, pzp=pzp):
+            for pyh in range(2):
+                there = (pzh * 8 + qx * 2 + qc, pyh * 32 + qy * 8 + pzp * 2 + qz)
+                pl.semaphore_signal(ready.at[zh], inc=1, device_id=there, device_id_type=MESH)
+
     loads[2].wait()
     v1 = chosen[0, 1]
     t0 = lax.dot_general(brv1[v1, 0], zq, (((0,), (0,)), ((), ())), preferred_element_type=F32)
@@ -168,33 +197,33 @@
     ]
     sendbuf[...] = jnp.concatenate(halves, axis=1).astype(BF)
 
-    pl.semaphore_wait(barrier, due)
-
-    mine = x * 2 + co
-
     slot = mine * 8 + yy * 2 + zz
-    for dx, dc in ((2, 1), (2, 0), (1, 1), (1, 0), (3, 1), (3, 0), (0, 1)):
-        pltpu.make_async_remote_copy(
-            src_ref=flag, dst_ref=flags.at[mine], send_sem=sendf, recv_sem=gotf,
-            device_id=(cut_of[dx][dc], stem_of[0][0]), device_id_type=MESH,
-        ).start()
     halves_of = [px // 2 for px in xs]
     cols = [[4 * pc + 2 * (px - 2 * half) + 1 for pc in cs] for px, half in zip(xs, halves_of)]
     rows_of = [lax.rem(py + 2, 8) * 8 for py in ys]
     flips = [lax.rem(py + 6, 8) * 8 - row for py, row in zip(ys, rows_of)]
-    for dx, dy, dc, dz in mates:
-        theirs = rows_of[dy] + halves_of[dx] * flips[dy] + cols[dx][dc] - zs[dz]
-        pltpu.make_async_remote_copy(
-            src_ref=sendbuf.at[theirs], dst_ref=recv1.at[slot], send_sem=send1, recv_sem=got1.at[dx],
-            device_id=(cut_of[dx][dc], stem_of[dy][dz]), device_id_type=MESH,
-        ).start()
-    for pzh, pzp, there_z in source_z:
-
-        @pl.when(there_z < height)
-        def _(pzh=pzh, pzp=pzp):
-            for pyh in range(2):
-                there = (pzh * 8 + qx * 2 + qc, pyh * 32 + qy * 8 + pzp * 2 + qz)
-                pl.semaphore_signal(ready.at[zh], inc=1, device_id=there, device_id_type=MESH)
+
+    def send_blocks(dy, group_of_mates):
+        for dx, dc, dz in group_of_mates:
+            theirs = rows_of[dy] + halves_of[dx] * flips[dy] + cols[dx][dc] - zs[dz]
+            pltpu.make_async_remote_copy(
+                src_ref=sendbuf.at[theirs], dst_ref=recv1.at[slot], send_sem=send1, recv_sem=got1.at[dx],
+                device_id=(cut_of[dx][dc], stem_of[dy][dz]), device_id_type=MESH,
+            ).start()
+
+    for dy in (2, 1, 3):
+
+        @pl.when(rank_of[dy] < rank_of[0])
+        def _(dy=dy):
+            send_blocks(dy, crowd)
+
+    send_blocks(0, crowd[:-1])
+    for dy in (2, 1, 3):
+
+        @pl.when(rank_of[dy] > rank_of[0])
+        def _(dy=dy):
+            pl.semaphore_wait(open1.at[dy], 16)
+            send_blocks(dy, crowd)
 
     recv1[slot] = sendbuf[group]
     flags[mine] = flag[...]
@@ -288,6 +317,7 @@
             pltpu.SemaphoreType.DMA,
             pltpu.SemaphoreType.DMA,
             pltpu.SemaphoreType.REGULAR((2,)),
+            pltpu.SemaphoreType.REGULAR((4,)),
         ],
         compiler_params=pltpu.CompilerParams(collective_id=0, has_side_effects=True),
     )(slice_values, mode_perms, owner_map, stems.reshape(128, 2, 512), branches, closing)

time: 43 us -> 48.3 us (1.12)
  the two profiles are of different devices: /device:TPU:1 before, /device:TPU:64 now
where the time goes in v4:
time: 48.3 us; the launch traced here: 48.1 us
  Pallas kernels  46.7 us (97%)
  local copies, waits for them, and re-layouts  1.32 us (3%)
    pallas_call x1, Pallas kernels, body(): pl.pallas_call(kernel, out_shape=jax.ShapeDtypeStruct((2, 16, 128), F32),...  46.7 us
    unnamed x1, local copies, waits for them, and re-layouts  1.32 us

profile of v4, /device:TPU:64, one launch (start us, length us, event | category | flops | bytes accessed | tf_op | source)
XLA Modules:
  0.0 48.1 jit_solution(10445923739688150205)
XLA Ops:
  0.0 46.7 %shard_map.64 = f32[2,16,128]{2,1,0:T(8,128)} custom-call(s32[1,3]{1,0:T(1,128)} %chosen_hbm.1, s32[3,9]{1,0:T(4,128)} %perms_hbm.1, s32[16]{0:T(128)} %owners_hbm.1, bf16[128,2,512]{2,1,0:T(2,128)(2,1)} %bitcast.2, bf16[2,2,2,512,512]{4,3,2,1,0:T(8,128)(2,1)} %br_hbm.1, bf16[2,2,512,256]{3,2,1,0:T(8,128)(2,1)} %cl_hbm.1), custom_call_target="tpu_custom_call" | custom-call | tf_op jit(solution)/shard_map/pallas_call | solution.py:292
  46.8 1.3 %copy.8 = f32[1,1,2,16,128]{4,3,2,1,0:T(8,128)} copy(f32[1,1,2,16,128]{4,3,2,1,0:T(8,128)} %bitcast.3) | data formatting | bytes 32768

commit v5 on v3

--- a/solution.py
+++ b/solution.py
@@ -262,7 +262,7 @@
     hbm = pl.BlockSpec(memory_space=pl.ANY)
     out = pl.pallas_call(
         kernel,
-        out_shape=jax.ShapeDtypeStruct((2, 16, 128), F32),
+        out_shape=pltpu.VMEM((2, 16, 128), F32),
         in_specs=[hbm] * 6,
         out_specs=pl.BlockSpec(memory_space=pltpu.VMEM),
         scratch_shapes=[

time: 43 us -> 41.6 us (0.967)
  local copies, waits for them, and re-layouts: 1.32 us -> 0.61 us
  Pallas kernels: 41.4 us -> 40.9 us
    unnamed x1, local copies, waits for them, and re-layouts: 1.32 us -> 0.61 us
    pallas_call x1, Pallas kernels: 41.4 us -> 40.9 us  [body(): pl.pallas_call(kernel, out_shape=pltpu.VMEM((2, 16, 128), F32), in_specs=...]
where the time goes in v5:
time: 41.6 us; the launch traced here: 41.5 us
  Pallas kernels  40.9 us (98%)
  local copies, waits for them, and re-layouts  0.61 us (1%)
    pallas_call x1, Pallas kernels, body(): pl.pallas_call(kernel, out_shape=pltpu.VMEM((2, 16, 128), F32), in_specs=...  40.9 us

profile of v5, /device:TPU:1, one launch (start us, length us, event | category | flops | bytes accessed | tf_op | source)
XLA Modules:
  0.0 41.5 jit_solution(9031092417185458589)
XLA Ops:
  0.0 40.9 %shard_map.64 = f32[2,16,128]{2,1,0:T(8,128)S(1)} custom-call(s32[1,3]{1,0:T(1,128)} %chosen_hbm.1, s32[3,9]{1,0:T(4,128)} %perms_hbm.1, s32[16]{0:T(128)} %owners_hbm.1, bf16[128,2,512]{2,1,0:T(2,128)(2,1)} %bitcast.3, bf16[2,2,2,512,512]{4,3,2,1,0:T(8,128)(2,1)} %br_hbm.1, bf16[2,2,512,256]{3,2,1,0:T(8,128)(2,1)} %cl_hbm.1), custom_call_target="tpu_custom_call" | custom-call | tf_op jit(solution)/shard_map/pallas_call | solution.py:263
  40.9 0.6 %copy.8 = f32[1,1,2,16,128]{4,3,2,1,0:T(8,128)} copy(f32[1,1,2,16,128]{4,3,2,1,0:T(8,128)S(1)} %bitcast.2) | data formatting | bytes 32768
